TPU v7x, 32 devices: a whole 2x2x4 slice. The times are simulated.
32 devices in a mesh: dp: 8 (over y, x, core), seq: 4 (over z).
Axes of the slice: x: 2, y: 2, z: 4, core: 2. Of those that a mesh axis runs over, the one named last changes fastest.
Arguments:
- student_in: bfloat16 [4096, 3584], P(('dp', 'seq')), may hold values from -6 to 6
- weight: bfloat16 [3584, 512], P(('dp', 'seq')), may hold values from -0.09375 to 0.09375
- queries: bfloat16 [4096, 512], P(('dp', 'seq')), may hold values from -8 to 8, as said below
- keys: bfloat16 [4096, 128], P(('dp', 'seq')), may hold values from -8 to 8
- values: bfloat16 [4096, 128], P(('dp', 'seq')), may hold values from -6 to 6
- lengths: int32 [8, 4], P('dp'), may hold values from 1 to 384, 512 in all within a row
- assignment: int32 [8, 4], P('dp'), may hold values from 0 to 3, each once within a row
Outputs:
- attention: bfloat16 [4096, 512], P(('dp', 'seq'))
- weight_grad: float32 [3584, 512], P(('dp', 'seq'))
Inputs may be any that keep to these rules, and one draw needn't show every extreme that they name: `queries`: entries of head 0 and of keys may reach the ends of this range. Each row holds the lengths of 4 rollouts of one sequence, summing to 512, the longest exactly 384. `assignment`: each row is a permutation of the 4 rollout blocks of one sequence.
All inputs are finite; a program needn't handle non-finite values.
Results may differ from a plain program's by a relative error of at most 0.012.
Values may be sent and summed in bfloat16 or wider, within the bound.
A program may use at most 64 MiB of HBM per device.

v0:
```python
import math

import jax
import jax.numpy as jnp
from jax import lax
from jax.sharding import PartitionSpec as P

HD = 128
HQ = 4
BLK = 128


EPSILON = 1e-06
NEGATIVE = -1e30


def locate(assign_row, doc_ends, first_slot, count):
    slot_ids = first_slot + jnp.arange(count, dtype=jnp.int32)
    block_ids = slot_ids // BLK
    block_table = jnp.arange(assign_row.shape[0], dtype=jnp.int32)
    placed = jnp.sum(
        jnp.where(block_ids[:, None] == block_table[None, :], assign_row[None, :], 0), axis=1
    )
    position = placed * BLK + slot_ids % BLK
    document = jnp.sum((position[:, None] >= doc_ends[None, :]).astype(jnp.int32), axis=1)
    return (position, document)


def absorb_block(state, key_block, value_block, query_heads, allowed):
    run_max, run_total, run_acc = state
    scores = jnp.einsum(
        "qhd,kd->hqk", query_heads, key_block, preferred_element_type=jnp.float32
    ) * HD ** (-0.5)
    masked = jnp.where(allowed[None], scores, NEGATIVE)
    new_max = jnp.maximum(run_max, jnp.max(masked, axis=-1))
    fading = jnp.exp(run_max - new_max)
    exp_terms = jnp.where(allowed[None], jnp.exp(masked - new_max[:, :, None]), 0.0)
    new_total = run_total * fading + jnp.sum(exp_terms, axis=-1)
    mixture = jnp.einsum(
        "hqk,kd->qhd",
        exp_terms.astype(jnp.bfloat16),
        value_block,
        preferred_element_type=jnp.float32,
    )
    new_acc = run_acc * fading.T[:, :, None] + mixture
    return (new_max, new_total, new_acc)


def local(student_in, weight, queries, keys, values, lengths, assignment):
    rows = queries.shape[0]
    assign_row = assignment[0]
    doc_ends = jnp.cumsum(lengths[0])
    query_pos, query_doc = locate(assign_row, doc_ends, lax.axis_index("seq") * rows, rows)
    query_heads = queries.reshape(rows, HQ, HD)
    start_state = (
        jnp.full((HQ, rows), NEGATIVE, jnp.float32),
        jnp.zeros((HQ, rows), jnp.float32),
        jnp.zeros((rows, HQ, HD), jnp.float32),
    )
    key_piece = lax.all_gather(keys, "seq", axis=0, tiled=True)
    value_piece = lax.all_gather(values, "seq", axis=0, tiled=True)
    count = key_piece.shape[0]
    step_rows = math.gcd(count, 512)
    steps_count = count // step_rows
    key_pos, key_doc = locate(assign_row, doc_ends, jnp.int32(0), count)

    def one_step(running, slabs):
        key_block, value_block, key_position, key_document = slabs
        allowed = (query_doc[:, None] == key_document[None, :]) & (
            query_pos[:, None] >= key_position[None, :]
        )
        updated = absorb_block(running, key_block, value_block, query_heads, allowed)
        return (updated, None)

    slabs = (
        key_piece.reshape(steps_count, step_rows, HD),
        value_piece.reshape(steps_count, step_rows, HD),
        key_pos.reshape(steps_count, step_rows),
        key_doc.reshape(steps_count, step_rows),
    )
    result, _ = lax.scan(one_step, start_state, slabs)
    final_max, final_total, final_acc = result
    attention = (final_acc / final_total.T[:, :, None]).reshape(rows, HQ * HD).astype(jnp.bfloat16)
    as_float = student_in.astype(jnp.float32)
    normed = (
        as_float * lax.rsqrt(jnp.mean(as_float * as_float, axis=1, keepdims=True) + EPSILON)
    ).astype(jnp.bfloat16)
    group_rows = lax.all_gather(weight, "seq", axis=0, tiled=True)
    columns = normed
    predicted = jnp.dot(
        columns,
        lax.all_gather(group_rows, "dp", axis=0, tiled=True),
        preferred_element_type=jnp.float32,
    )
    dp_count = lax.axis_size("dp")
    seq_count = lax.axis_size("seq")
    token_total = rows * dp_count * seq_count
    scaled = ((predicted - attention.astype(jnp.float32)) * token_total ** (-0.5)).astype(
        jnp.bfloat16
    )
    columns = normed
    outer_rows = lax.psum_scatter(
        lax.dot_general(
            columns, scaled, (((0,), (0,)), ((), ())), preferred_element_type=jnp.float32
        ).astype(jnp.bfloat16),
        "dp",
        scatter_dimension=0,
        tiled=True,
    )
    weight_grad = lax.psum_scatter(outer_rows, "seq", scatter_dimension=0, tiled=True).astype(
        jnp.float32
    )
    return (attention, weight_grad)


def solution(mesh):
    placed = (
        P(("dp", "seq"), None),
        P(("dp", "seq"), None),
        P(("dp", "seq"), None),
        P(("dp", "seq"), None),
        P(("dp", "seq"), None),
        P("dp", None),
        P("dp", None),
    )
    return jax.shard_map(
        local,
        mesh=mesh,
        in_specs=placed,
        out_specs=(P(("dp", "seq"), None), P(("dp", "seq"), None)),
        check_vma=False,
    )
```

profile of v0, /device:TPU:0, one launch (start us, length us, event | category | flops | bytes accessed | tf_op | source)
XLA Modules:
  0.0 149.0 jit_solution(12489444883028070864)
XLA Ops:
  7.2 0.0 all-gather.2.cloned.1.call-start
  7.2 18.8 %all_gather.14 = bf16[448,512]{1,0:T(8,128)(2,1)} all-gather(bf16[112,512]{1,0:T(8,128)(2,1)} %param.8), channel_id=1, replica_groups=mesh['dp'=8,'seq'=4] {'seq'}, dimensions={0}, use_global_device_ids=true | all-gather | bytes 573440 | tf_op jit(solution)/shard_map/all_gather | solution.py:88
  26.0 0.0 all-gather.2.cloned.1.call-update
  26.0 0.0 reduce-scatter.3.cloned.1.call-start
  26.1 0.9 copy.14
  26.9 0.8 reduce-window.8
  27.8 12.3 %all_gather.13 = bf16[512,128]{0,1:T(8,128)(2,1)S(1)} all-gather(bf16[128,128]{0,1:T(8,128)(2,1)S(1)} %copy.14), channel_id=1, replica_groups=mesh['dp'=8,'seq'=4] {'seq'}, dimensions={0}, use_global_device_ids=true | all-gather | bytes 163840 | tf_op jit(solution)/shard_map/all_gather | solution.py:61
  40.1 13.5 %all_gather.12 = bf16[512,128]{1,0:T(8,128)(2,1)S(1)} all-gather(bf16[128,128]{1,0:T(8,128)(2,1)} %param.10), channel_id=1, replica_groups=mesh['dp'=8,'seq'=4] {'seq'}, dimensions={0}, use_global_device_ids=true | all-gather | bytes 163840 | tf_op jit(solution)/shard_map/all_gather | solution.py:60
  53.7 0.7 select_reduce_fusion.1
  54.5 0.1 convert_reduce_fusion.1
  54.5 0.7 select_reduce_fusion
  55.3 0.1 convert_reduce_fusion
  55.4 1.4 fusion
  56.8 0.2 compare_and_fusion
  57.1 0.3 fusion.36
  57.4 0.2 fusion.13
  57.6 0.3 fusion.8
  58.0 2.6 %all-gather.2.cloned.1.call-done = bf16[3584,512]{1,0:T(8,128)(2,1)} async-done(((bf16[448,512]{1,0:T(8,128)(2,1)}), bf16[3584,512]{1,0:T(8,128)(2,1)}) %all-gather.2.cloned.1.call-update) | async-done | bytes 3670032 | tf_op jit(solution)/shard_map/all_gather | solution.py:92
  60.6 7.9 %convolution_convert_fusion = bf16[3584,512]{1,0:T(8,128)(2,1)} fusion(bf16[3584,512]{1,0:T(8,128)(2,1)} %all-gather.2.cloned.1.call-done, bf16[128,3584]{1,0:T(8,128)(2,1)S(1)} %copy-done.1, f32[128]{0:T(128)S(1)} %add_rsqrt_fusion, bf16[128,512]{0,1:T(8,128)(2,1)S(1)} %bitcast.40), kind=kOutput, calls=%fused_computation | convolution fusion | flops 944373760 | bytes 8389120 | tf_op jit(solution)/shard_map/dot_general | solution.py:103
  68.6 0.0 reduce-scatter.5.cloned.1.call-start
  68.6 48.7 %reduce-scatter.3.cloned.1.call-done = bf16[448,512]{1,0:T(8,128)(2,1)} async-done(((bf16[3584,512]{1,0:T(8,128)(2,1)}), bf16[448,512]{1,0:T(8,128)(2,1)}) %reduce-scatter.3.cloned.1.call-update) | async-done | bytes 458768 | tf_op jit(solution)/shard_map/reduce_scatter | solution.py:102
  117.3 0.8 copy.16
  118.1 22.8 %reduce-scatter.5.cloned.1.call-done = bf16[112,512]{1,0:T(8,128)(2,1)} async-done(((bf16[448,512]{1,0:T(8,128)(2,1)}), bf16[112,512]{1,0:T(8,128)(2,1)}) %reduce-scatter.5.cloned.1.call-update) | async-done | bytes 114704 | tf_op jit(solution)/shard_map/reduce_scatter | solution.py:110
  140.9 1.6 %convert_element_type.44 = f32[112,512]{1,0:T(8,128)} convert(bf16[112,512]{1,0:T(8,128)(2,1)} %reduce-scatter.5.cloned.1.call-done) | non-fusion elementwise | flops 57344 | bytes 344064 | tf_op jit(solution)/shard_map/convert_element_type | solution.py:110
  (13 shorter events, 0.1 us)
Async XLA Ops:
  7.2 49.9 %copy-start = (bf16[128,512]{1,0:T(8,128)(2,1)S(1)}, bf16[128,512]{1,0:T(8,128)(2,1)}, u32[]{:S(2)}) copy-start(bf16[128,512]{1,0:T(8,128)(2,1)} %param.9) | copy-start | bytes 393220
  7.2 53.4 %copy-start.1 = (bf16[128,3584]{1,0:T(8,128)(2,1)S(1)}, bf16[128,3584]{1,0:T(8,128)(2,1)}, u32[]{:S(2)}) copy-start(bf16[128,3584]{1,0:T(8,128)(2,1)} %param.7) | copy-start | bytes 2752516
  7.2 53.4 %all-gather.2.cloned.1.call-start = ((), (), s32[]{:S(2)}) async-start(), calls=%async_computation.2 | async-start | bytes 4128768 | tf_op jit(solution)/shard_map/all_gather | solution.py:92
  26.0 91.3 %reduce-scatter.3.cloned.1.call-start = ((), (), s32[]{:S(2)}) async-start(), calls=%async_computation.3 | async-start | bytes 4128768 | tf_op jit(solution)/shard_map/reduce_scatter | solution.py:102
  68.6 72.3 %reduce-scatter.5.cloned.1.call-start = ((), (), s32[]{:S(2)}) async-start(), calls=%async_computation.4 | async-start | bytes 573440 | tf_op jit(solution)/shard_map/reduce_scatter | solution.py:110
Sparse Core Ops, SparseCore 0:
  26.1 34.3 all-gather.1
  68.7 48.5 reduce-scatter.2
  119.6 21.2 reduce-scatter.4
where the time goes:
time: 149 us
  waiting for transfers between devices  74.2 us (50%)
  blocking collectives  44.7 us (30%)
  between operations  13.8 us (9%)
  matrix products  8.59 us (6%)
  other arithmetic  6.01 us (4%)
  local copies, waits for them, and re-layouts  1.65 us (1%)
    reduce_scatter x1, waiting for transfers between devices, local(): lax.psum_scatter(lax.dot_general(columns, scaled, (((0,), (0,)), ((), ())...  48.7 us
    reduce_scatter x1, waiting for transfers between devices, local(): lax.psum_scatter(outer_rows, 'seq', scatter_dimension=0, tiled=True)  22.8 us
    all_gather x1, blocking collectives, local(): group_rows = lax.all_gather(weight, 'seq', axis=0, tiled=True)  18.8 us
    all_gather x1, blocking collectives, local(): key_piece = lax.all_gather(keys, 'seq', axis=0, tiled=True)  13.5 us
    all_gather x1, blocking collectives, local(): value_piece = lax.all_gather(values, 'seq', axis=0, tiled=True)  12.3 us
    dot_general x1, matrix products, local(): lax.dot_general(columns, scaled, (((0,), (0,)), ((), ())), preferred_elem...  7.94 us
  transfers between devices with their start and end apart: 3, of which 3 were waited for; matrix products, arithmetic and copies ran while one was open for 4% of the time, Pallas kernels for 0%

commit v1 on v0

--- a/solution.py
+++ b/solution.py
@@ -1,8 +1,11 @@
+import functools
 import math
 
 import jax
 import jax.numpy as jnp
 from jax import lax
+from jax.experimental import pallas as pl
+from jax.experimental.pallas import tpu as pltpu
 from jax.sharding import PartitionSpec as P
 
 HD = 128
@@ -113,6 +116,341 @@
     return (attention, weight_grad)
 
 
+MESH = pl.DeviceIdType.MESH
+F32 = jnp.float32
+BF16 = jnp.bfloat16
+
+
+def fused_kernel(
+    token_total,
+    x_ref, w_ref, q_ref, k_ref, v_ref, len_ref, asg_ref,
+    att_ref, out_ref,
+    x_peer, w_all, kv_all, xn, xt, pred, att_half, att_peer,
+    own_f, gx_f, gy_f, s_d, s_x, s_y, s_z, r_dx, r_dy, r_x, r_y, r_z,
+    send, sem_w, sem_kv, sem_x, sem_att, sem_dx, sem_dy, sem_rx, sem_ry, sem_rz,
+):
+    rows = q_ref.shape[0]
+    piece = w_ref.shape[0]
+    half = w_ref.shape[1] // 2
+    depth = xn.shape[2]
+    dp, z = lax.axis_index("dp"), lax.axis_index("seq")
+    c = dp % 2
+    pc = 1 - c
+    x = (dp // 2) % 2
+    y = dp // 4
+    q = dp // 2
+    qx, qy, qd = y * 2 + 1 - x, (1 - y) * 2 + x, 3 - q
+    mate = (dp + 1 - 2 * c, z)
+    xn_dev = (dp + 2 - 4 * x, z)
+    yn_dev = (dp + 4 - 8 * y, z)
+    zs = (z, z + 1 - 2 * (z % 2), z + 2 - 4 * (z // 2), 3 - z)
+    z_dev = [(dp, zs[r]) for r in range(4)]
+    z_mate = [(dp + 1 - 2 * c, zs[r]) for r in range(4)]
+
+    peers = [mate, xn_dev, yn_dev] + z_dev[1:] + z_mate[1:]
+    barrier = pltpu.get_barrier_semaphore()
+    for dev in peers:
+        pl.semaphore_signal(barrier, inc=1, device_id=dev, device_id_type=MESH)
+    pl.semaphore_wait(barrier, len(peers))
+
+    sent = []
+
+    def push(src, dst, rsem, dev):
+        copy = pltpu.make_async_remote_copy(
+            src_ref=src, dst_ref=dst, send_sem=send.at[len(sent)], recv_sem=rsem,
+            device_id=dev, device_id_type=MESH,
+        )
+        copy.start()
+        sent.append(copy)
+
+    def arrive(dst, rsem):
+        pltpu.make_async_remote_copy(
+            src_ref=dst, dst_ref=dst, send_sem=send.at[0], recv_sem=rsem,
+            device_id=mate, device_id_type=MESH,
+        ).wait_recv()
+
+    def cols(core):
+        return pl.ds(pl.multiple_of(core * half, 128), half)
+
+    def w_push(at, dev):
+        push(w_all.at[at], w_all.at[at], sem_w.at[at], dev)
+
+    def w_arrive(at):
+        arrive(w_all.at[at], sem_w.at[at])
+
+    mine, other = (q, c, z), (q, pc, z)
+    own_half = w_ref.at[:, cols(c)]
+    push(w_ref.at[:, cols(pc)], w_all.at[mine], sem_w.at[mine], mate)
+    for dev in (z_dev[1], xn_dev, yn_dev):
+        push(own_half, w_all.at[mine], sem_w.at[mine], dev)
+    push(x_ref, x_peer, sem_x.at[0], mate)
+    w_all[mine] = w_ref[:, cols(c)]
+    w_arrive(other)
+    for dev in (z_dev[1], xn_dev, yn_dev):
+        w_push(other, dev)
+    for r in (2, 3):
+        push(own_half, w_all.at[mine], sem_w.at[mine], z_dev[r])
+        w_push(other, z_dev[r])
+        if r == 2:
+            kv_push_order = (1,)
+        else:
+            kv_push_order = (2, 3)
+        for s in kv_push_order:
+            push(k_ref, kv_all.at[0, z], sem_kv.at[0, z], z_dev[s])
+            push(v_ref, kv_all.at[1, z], sem_kv.at[1, z], z_dev[s])
+    kv_all[0, z] = k_ref[...]
+    kv_all[1, z] = v_ref[...]
+
+    step = 16
+
+    def norm_rows(source, base):
+        @pl.loop(0, rows // step)
+        def _(i):
+            at = pl.multiple_of(i * step, step)
+            block = source[pl.ds(at, step), :].astype(F32)
+            normed = (
+                block * lax.rsqrt(jnp.mean(block * block, axis=1, keepdims=True) + EPSILON)
+            ).astype(BF16)
+            for part in range(4):
+                xn[part, pl.ds(pl.multiple_of(base + at, step), step), :] = normed[
+                    :, part * depth : (part + 1) * depth
+                ]
+
+    def relay(r):
+        w_arrive((qx, 0, zs[r]))
+        w_push((qx, 0, zs[r]), yn_dev)
+        w_arrive((qy, 1, zs[r]))
+        w_push((qy, 1, zs[r]), xn_dev)
+
+    def forward(r):
+        for part in range(2):
+            at = (q, part, zs[r])
+            w_arrive(at)
+            w_push(at, xn_dev)
+            w_push(at, yn_dev)
+
+    def w_block(at):
+        return w_all[at].reshape(depth, half)
+
+    norm_rows(x_ref, 0)
+    relay(0)
+    forward(1)
+    arrive(x_peer, sem_x.at[0])
+    norm_rows(x_peer, rows)
+    forward(2)
+    relay(1)
+
+    @pl.loop(0, 4)
+    def _(part):
+        for j in range(depth // 128):
+            xt[part, j * 128 : (j + 1) * 128, :] = xn[part, :, j * 128 : (j + 1) * 128].T
+
+    forward(3)
+    relay(2)
+    pred[...] = jnp.dot(xn[q], w_block(q), preferred_element_type=F32)
+
+    for r in range(1, 4):
+        for part in range(2):
+            arrive(kv_all.at[part, zs[r]], sem_kv.at[part, zs[r]])
+    ends = []
+    total = 0
+    for i in range(len_ref.shape[1]):
+        total = total + len_ref[0, i]
+        ends.append(total)
+
+    def document(position):
+        found = jnp.zeros(position.shape, jnp.int32)
+        for end in ends:
+            found = found + (position >= end).astype(jnp.int32)
+        return found
+
+    lanes = lax.broadcasted_iota(jnp.int32, (1, BLK), 1)
+    k_pos = jnp.concatenate([asg_ref[0, j] * BLK + lanes for j in range(4)], axis=1)
+    q_pos = asg_ref[0, z] * BLK + lax.broadcasted_iota(jnp.int32, (rows, 1), 0)
+    allowed = (document(q_pos) == document(k_pos)) & (q_pos >= k_pos)
+    k_all = kv_all[0].reshape(4 * rows, HD)
+    v_all = kv_all[1].reshape(4 * rows, HD)
+    for h in range(HQ):
+        scores = lax.dot_general(
+            q_ref[:, h * HD : (h + 1) * HD], k_all, (((1,), (1,)), ((), ())),
+            preferred_element_type=F32,
+        ) * HD ** (-0.5)
+        masked = jnp.where(allowed, scores, NEGATIVE)
+        top = jnp.max(masked, axis=1, keepdims=True)
+        terms = jnp.where(allowed, jnp.exp(masked - top), 0.0)
+        totals = jnp.sum(terms, axis=1, keepdims=True)
+        mixture = jnp.dot(terms.astype(BF16), v_all, preferred_element_type=F32)
+        done = (mixture / totals).astype(BF16)
+        att_ref[:, h * HD : (h + 1) * HD] = done
+        place = (h % 2) * HD
+        att_half[h // 2, :, place : place + HD] = done
+    push(att_half.at[pc], att_peer, sem_att.at[0], mate)
+    relay(3)
+
+    for r in range(4):
+        w_arrive((qx, 1, zs[r]))
+    pred[...] += jnp.dot(xn[qx], w_block(qx), preferred_element_type=F32)
+    for r in range(4):
+        w_arrive((qy, 0, zs[r]))
+    pred[...] += jnp.dot(xn[qy], w_block(qy), preferred_element_type=F32)
+    arrive(att_peer, sem_att.at[0])
+    for r in range(4):
+        for part in range(2):
+            w_arrive((qd, part, zs[r]))
+    predicted = pred[...] + jnp.dot(xn[qd], w_block(qd), preferred_element_type=F32)
+    attended = jnp.concatenate([att_half[c], att_peer[...]], axis=0).astype(F32)
+    scaled = ((predicted - attended) * token_total ** (-0.5)).astype(BF16)
+
+    def grad(at):
+        return jnp.dot(xt[at], scaled, preferred_element_type=F32).reshape(2, 4, piece, half)
+
+    def send_diagonal(g):
+        push(s_d.at[0, g], r_dy.at[g], sem_dy.at[g], yn_dev)
+        push(s_d.at[1, g], r_dx.at[g], sem_dx.at[g], xn_dev)
+
+    def send_direct(g):
+        push(s_x.at[1, g], r_x.at[1, g], sem_rx.at[1, g], xn_dev)
+        push(s_y.at[0, g], r_y.at[0, g], sem_ry.at[0, g], yn_dev)
+
+    def send_joined(g):
+        arrive(r_dy.at[g], sem_dy.at[g])
+        s_x[0, g] = (gx_f[g] + r_dy[g].astype(F32)).astype(BF16)
+        push(s_x.at[0, g], r_x.at[0, g], sem_rx.at[0, g], xn_dev)
+        arrive(r_dx.at[g], sem_dx.at[g])
+        s_y[1, g] = (gy_f[g] + r_dx[g].astype(F32)).astype(BF16)
+        push(s_y.at[1, g], r_y.at[1, g], sem_ry.at[1, g], yn_dev)
+
+    def column_sum(part, g):
+        arrive(r_x.at[part, g], sem_rx.at[part, g])
+        arrive(r_y.at[part, g], sem_ry.at[part, g])
+        return own_f[part, g] + r_x[part, g].astype(F32) + r_y[part, g].astype(F32)
+
+    def send_column(r):
+        g = zs[r]
+        for part in range(2):
+            s_z[part, g] = column_sum(part, g).astype(BF16)
+        push(s_z.at[c, g], r_z.at[z, c], sem_rz.at[z, c], z_dev[r])
+        push(s_z.at[pc, g], r_z.at[z, c], sem_rz.at[z, c], z_mate[r])
+
+    order = (3, 2, 1, 0)
+    g = [zs[r] for r in order]
+    s_d[...] = grad(qd).astype(BF16)
+    send_diagonal(g[0])
+    send_diagonal(g[1])
+    block = grad(qx)
+    gx_f[...] = block[0]
+    s_x[1] = block[1].astype(BF16)
+    block = grad(qy)
+    gy_f[...] = block[1]
+    s_y[0] = block[0].astype(BF16)
+    send_direct(g[0])
+    own_f[...] = grad(q)
+    send_joined(g[0])
+    send_diagonal(g[2])
+    send_direct(g[1])
+    send_joined(g[1])
+    send_diagonal(g[3])
+    send_direct(g[2])
+    send_column(order[0])
+    send_joined(g[2])
+    send_direct(g[3])
+    send_column(order[1])
+    send_joined(g[3])
+    send_column(order[2])
+
+    for part in range(2):
+        own_f[part, z] = column_sum(part, z)
+    s_z[pc, z] = own_f[pc, z].astype(BF16)
+    push(s_z.at[pc, z], r_z.at[z, c], sem_rz.at[z, c], mate)
+    total = own_f[c, z]
+    for r in range(1, 4):
+        arrive(r_z.at[zs[r], c], sem_rz.at[zs[r], c])
+        total = total + r_z[zs[r], c].astype(F32)
+    out_ref[:, cols(c)] = total
+    total = jnp.zeros((piece, half), F32)
+    for r in (3, 2, 1, 0):
+        arrive(r_z.at[zs[r], pc], sem_rz.at[zs[r], pc])
+        total = total + r_z[zs[r], pc].astype(F32)
+    out_ref[:, cols(pc)] = total
+    for copy in sent:
+        copy.wait_send()
+
+
+def local_fused(student_in, weight, queries, keys, values, lengths, assignment):
+    rows, width = student_in.shape
+    piece, features = weight.shape
+    half = features // 2
+    depth = width // 4
+    token_total = rows * lax.axis_size("dp") * lax.axis_size("seq")
+    vmem = pl.BlockSpec(memory_space=pltpu.VMEM)
+    smem = pl.BlockSpec(memory_space=pltpu.SMEM)
+    dma = pltpu.SemaphoreType.DMA
+    quarter = (2, 4, piece, half)
+    return pl.pallas_call(
+        functools.partial(fused_kernel, token_total),
+        out_shape=(
+            jax.ShapeDtypeStruct((rows, features), BF16),
+            jax.ShapeDtypeStruct((piece, features), F32),
+        ),
+        in_specs=[vmem] * 5 + [smem] * 2,
+        out_specs=(vmem, vmem),
+        scratch_shapes=[
+            pltpu.VMEM((rows, width), BF16),
+            pltpu.VMEM((4,) + quarter, BF16),
+            pltpu.VMEM((2, 4, rows, HD), BF16),
+            pltpu.VMEM((4, 2 * rows, depth), BF16),
+            pltpu.VMEM((4, depth, 2 * rows), BF16),
+            pltpu.VMEM((2 * rows, half), F32),
+            pltpu.VMEM((2, rows, half), BF16),
+            pltpu.VMEM((rows, half), BF16),
+            pltpu.VMEM(quarter, F32),
+            pltpu.VMEM(quarter[1:], F32),
+            pltpu.VMEM(quarter[1:], F32),
+            pltpu.VMEM(quarter, BF16),
+            pltpu.VMEM(quarter, BF16),
+            pltpu.VMEM(quarter, BF16),
+            pltpu.VMEM(quarter, BF16),
+            pltpu.VMEM(quarter[1:], BF16),
+            pltpu.VMEM(quarter[1:], BF16),
+            pltpu.VMEM(quarter, BF16),
+            pltpu.VMEM(quarter, BF16),
+            pltpu.VMEM((4, 2, piece, half), BF16),
+            dma((80,)),
+            dma((4, 2, 4)),
+            dma((2, 4)),
+            dma((1,)),
+            dma((1,)),
+            dma((4,)),
+            dma((4,)),
+            dma((2, 4)),
+            dma((2, 4)),
+            dma((4, 2)),
+        ],
+        compiler_params=pltpu.CompilerParams(collective_id=0, has_side_effects=True),
+        name="distill",
+    )(student_in, weight, queries, keys, values, lengths, assignment)
+
+
+def fits(student_in, weight, queries, keys, values, lengths, assignment):
+    rows, width = student_in.shape
+    piece, features = weight.shape
+    return (
+        lax.axis_size("dp") == 8
+        and lax.axis_size("seq") == 4
+        and rows == BLK
+        and assignment.shape[1] == 4
+        and piece % 16 == 0
+        and width == 32 * piece
+        and width % 512 == 0
+        and features == HQ * HD
+        and keys.shape[1] == HD
+    )
+
+
+def dispatch(*arrays):
+    return local_fused(*arrays) if fits(*arrays) else local(*arrays)
+
+
 def solution(mesh):
     placed = (
         P(("dp", "seq"), None),
@@ -124,7 +462,7 @@
         P("dp", None),
     )
     return jax.shard_map(
-        local,
+        dispatch,
         mesh=mesh,
         in_specs=placed,
         out_specs=(P(("dp", "seq"), None), P(("dp", "seq"), None)),

time: 149 us -> 54.1 us (0.36)
  waiting for transfers between devices: 74.2 us -> 0 us
  Pallas kernels: 0 us -> 51 us
  blocking collectives: 44.7 us -> 0 us
  between operations: 13.8 us -> 0.65 us
  matrix products: 8.59 us -> 0 us
  other arithmetic: 6.01 us -> 0 us
    reduce_scatter x2 -> x0, waiting for transfers between devices: 71.5 us -> none  [the longest x1 48.7 us: local(): lax.psum_scatter(lax.dot_general(columns, scaled, (((0,), (0,)), ((), ())...]
    pallas_call x0 -> x1, Pallas kernels: none -> 51 us  [local_fused(): pl.pallas_call(functools.partial(fused_kernel, token_total), out_shape=(j...]
    all_gather x3 -> x0, blocking collectives: 44.7 us -> none  [the longest x1 18.8 us: local(): group_rows = lax.all_gather(weight, 'seq', axis=0, tiled=True)]
    dot_general x3 -> x0, matrix products: 8.59 us -> none  [the longest x1 7.94 us: local(): lax.dot_general(columns, scaled, (((0,), (0,)), ((), ())), preferred_elem...]
    reduce_sum x6 -> x0, other arithmetic: 3.31 us -> none  [the longest x2 1.48 us: locate(): jnp.sum(jnp.where(block_ids[:, None] == block_table[None, :], assign_row[...]
    all_gather x1 -> x0, waiting for transfers between devices: 2.63 us -> none  [local(): lax.all_gather(group_rows, 'dp', axis=0, tiled=True)]
    convert_element_type x1 -> x0, other arithmetic: 1.61 us -> none  [local(): lax.psum_scatter(outer_rows, 'seq', scatter_dimension=0, tiled=True)]
  transfers between devices with their start and end apart: 3 -> 0, of which waited for: 3 -> 0; matrix products, arithmetic and copies ran while one was open for 4% -> 0% of each run, Pallas kernels for 0% -> 0%
where the time goes in v1:
time: 54.1 us; the launch traced here: 53.9 us
  Pallas kernels  51 us (94%)
  local copies, waits for them, and re-layouts  2.3 us (4%)
  between operations  0.65 us (1%)
    pallas_call x1, Pallas kernels, local_fused(): pl.pallas_call(functools.partial(fused_kernel, token_total), out_shape=(j...  51 us
    unnamed x4, local copies, waits for them, and re-layouts  2.3 us

profile of v1, /device:TPU:0, one launch (start us, length us, event | category | flops | bytes accessed | tf_op | source)
XLA Modules:
  0.0 53.9 jit_solution(16607684273676147375)
XLA Ops:
  0.6 51.0 %distill.1 = (bf16[128,512]{1,0:T(8,128)(2,1)}, f32[112,512]{1,0:T(8,128)}) custom-call(bf16[128,3584]{1,0:T(8,128)(2,1)} %x_ref.1, bf16[112,512]{1,0:T(8,128)(2,1)} %w_ref.1, bf16[128,512]{1,0:T(8,128)(2,1)} %q_ref.1, bf16[128,128]{1,0:T(8,128)(2,1)} %k_ref.1, bf16[128,128]{1,0:T(8,128)(2,1)} %v_ref.1, s32[1,4]{1,0:T(1,128)} %len_ref.1, s32[1,4]{1,0:T(1,128)} %asg_ref.1), custom_call_target="tpu_custom_call" | custom-call | tf_op jit(solution)/shard_map/distill/pallas_call | solution.py:389
  51.6 0.0 copy-start
  51.6 1.6 %copy.11 = bf16[128,512]{1,0:T(8,128)(2,1)} copy(bf16[128,512]{1,0:T(8,128)(2,1)} %get-tuple-element.4) | data formatting | bytes 262144
  53.2 0.0 copy-done
  53.2 0.7 %copy.12 = f32[112,512]{1,0:T(8,128)} copy(f32[112,512]{1,0:T(8,128)S(1)} %copy-done) | data formatting | bytes 458752
Async XLA Ops:
  51.6 1.6 %copy-start = (f32[112,512]{1,0:T(8,128)S(1)}, f32[112,512]{1,0:T(8,128)}, u32[]{:S(2)}) copy-start(f32[112,512]{1,0:T(8,128)} %get-tuple-element.5) | copy-start | bytes 688132

commit v2 on v1

--- a/solution.py
+++ b/solution.py
@@ -125,21 +125,20 @@
     token_total,
     x_ref, w_ref, q_ref, k_ref, v_ref, len_ref, asg_ref,
     att_ref, out_ref,
-    x_peer, w_all, kv_all, xn, xt, pred, att_half, att_peer,
-    own_f, gx_f, gy_f, s_d, s_x, s_y, s_z, r_dx, r_dy, r_x, r_y, r_z,
-    send, sem_w, sem_kv, sem_x, sem_att, sem_dx, sem_dy, sem_rx, sem_ry, sem_rz,
+    xs, xt, w_all, kv_all, inv, pred, p_out, p_in, s_all, att_half, att_peer,
+    grad_f, s_y, r_y, s_z, r_z,
+    send, sem_w, sem_kv, sem_x, sem_inv, sem_att, sem_p, sem_s, sem_ry, sem_rz,
 ):
     rows = q_ref.shape[0]
     piece = w_ref.shape[0]
     half = w_ref.shape[1] // 2
-    depth = xn.shape[2]
+    depth = xs.shape[3]
     dp, z = lax.axis_index("dp"), lax.axis_index("seq")
     c = dp % 2
     pc = 1 - c
     x = (dp // 2) % 2
     y = dp // 4
-    q = dp // 2
-    qx, qy, qd = y * 2 + 1 - x, (1 - y) * 2 + x, 3 - q
+    yo = 1 - y
     mate = (dp + 1 - 2 * c, z)
     xn_dev = (dp + 2 - 4 * x, z)
     yn_dev = (dp + 4 - 8 * y, z)
@@ -172,82 +171,106 @@
     def cols(core):
         return pl.ds(pl.multiple_of(core * half, 128), half)
 
+    def width(at_y, at_x):
+        return pl.ds(pl.multiple_of((at_y * 2 + at_x) * depth, 128), depth)
+
     def w_push(at, dev):
         push(w_all.at[at], w_all.at[at], sem_w.at[at], dev)
 
     def w_arrive(at):
         arrive(w_all.at[at], sem_w.at[at])
 
-    mine, other = (q, c, z), (q, pc, z)
+    def x_push(at_y, at_x, slot, dev):
+        push(x_ref.at[:, width(at_y, at_x)], xs.at[at_y, slot], sem_x.at[at_y, slot], dev)
+
+    mine, other = (y, c, z), (y, pc, z)
     own_half = w_ref.at[:, cols(c)]
     push(w_ref.at[:, cols(pc)], w_all.at[mine], sem_w.at[mine], mate)
-    for dev in (z_dev[1], xn_dev, yn_dev):
-        push(own_half, w_all.at[mine], sem_w.at[mine], dev)
-    push(x_ref, x_peer, sem_x.at[0], mate)
+    push(own_half, w_all.at[mine], sem_w.at[mine], z_dev[1])
+    push(own_half, w_all.at[mine], sem_w.at[mine], yn_dev)
+    x_push(y, 1 - x, 2, xn_dev)
+    x_push(yo, 1 - x, 2, xn_dev)
+    x_push(y, x, 1, mate)
+    x_push(yo, x, 1, mate)
     w_all[mine] = w_ref[:, cols(c)]
     w_arrive(other)
-    for dev in (z_dev[1], xn_dev, yn_dev):
-        w_push(other, dev)
+    w_push(other, z_dev[1])
+    w_push(other, yn_dev)
     for r in (2, 3):
         push(own_half, w_all.at[mine], sem_w.at[mine], z_dev[r])
         w_push(other, z_dev[r])
-        if r == 2:
-            kv_push_order = (1,)
-        else:
-            kv_push_order = (2, 3)
-        for s in kv_push_order:
-            push(k_ref, kv_all.at[0, z], sem_kv.at[0, z], z_dev[s])
-            push(v_ref, kv_all.at[1, z], sem_kv.at[1, z], z_dev[s])
+    for r in (1, 2, 3):
+        push(k_ref, kv_all.at[0, z], sem_kv.at[0, z], z_dev[r])
+        push(v_ref, kv_all.at[1, z], sem_kv.at[1, z], z_dev[r])
     kv_all[0, z] = k_ref[...]
     kv_all[1, z] = v_ref[...]
+    xs[y, 0] = x_ref[:, width(y, x)]
+    xs[yo, 0] = x_ref[:, width(yo, x)]
 
     step = 16
 
-    def norm_rows(source, base):
-        @pl.loop(0, rows // step)
-        def _(i):
-            at = pl.multiple_of(i * step, step)
-            block = source[pl.ds(at, step), :].astype(F32)
-            normed = (
-                block * lax.rsqrt(jnp.mean(block * block, axis=1, keepdims=True) + EPSILON)
-            ).astype(BF16)
-            for part in range(4):
-                xn[part, pl.ds(pl.multiple_of(base + at, step), step), :] = normed[
-                    :, part * depth : (part + 1) * depth
-                ]
-
-    def relay(r):
-        w_arrive((qx, 0, zs[r]))
-        w_push((qx, 0, zs[r]), yn_dev)
-        w_arrive((qy, 1, zs[r]))
-        w_push((qy, 1, zs[r]), xn_dev)
+    @pl.loop(0, rows // step)
+    def _(i):
+        at = pl.ds(pl.multiple_of(i * step, step), step)
+        block = x_ref[at, :].astype(F32)
+        factor = lax.rsqrt(jnp.mean(block * block, axis=1, keepdims=True) + EPSILON)
+        inv[0, at, :] = jnp.broadcast_to(factor, (step, 128))
+
+    push(inv.at[0], inv.at[1], sem_inv.at[0], mate)
 
     def forward(r):
         for part in range(2):
-            at = (q, part, zs[r])
+            at = (y, part, zs[r])
             w_arrive(at)
-            w_push(at, xn_dev)
             w_push(at, yn_dev)
 
-    def w_block(at):
-        return w_all[at].reshape(depth, half)
-
-    norm_rows(x_ref, 0)
-    relay(0)
+    def x_arrive(at_y, slot):
+        arrive(xs.at[at_y, slot], sem_x.at[at_y, slot])
+
+    def x_relay(at_y):
+        x_arrive(at_y, 2)
+        push(xs.at[at_y, 2], xs.at[at_y, 3], sem_x.at[at_y, 3], mate)
+
+    def turn(at_y, slot):
+        for j in range(depth // 128):
+            at = slice(j * 128, (j + 1) * 128)
+            xt[at_y, at, slot * rows : (slot + 1) * rows] = xs[at_y, slot, :, at].T
+
+    def w_block(at_y):
+        return w_all[at_y].reshape(depth, half)
+
+    def product(at_y, first):
+        return jnp.dot(
+            xs[at_y, first : first + 2].reshape(2 * rows, depth), w_block(at_y),
+            preferred_element_type=F32,
+        )
+
     forward(1)
-    arrive(x_peer, sem_x.at[0])
-    norm_rows(x_peer, rows)
+    x_arrive(y, 1)
+    x_arrive(yo, 1)
+    for slot in range(2):
+
+        @pl.loop(0, 2)
+        def _(at_y):
+            turn(at_y, slot)
+
     forward(2)
-    relay(1)
-
-    @pl.loop(0, 4)
-    def _(part):
-        for j in range(depth // 128):
-            xt[part, j * 128 : (j + 1) * 128, :] = xn[part, :, j * 128 : (j + 1) * 128].T
-
+    x_relay(y)
     forward(3)
-    relay(2)
-    pred[...] = jnp.dot(xn[q], w_block(q), preferred_element_type=F32)
+    pred[0] = product(y, 0)
+    x_relay(yo)
+    x_arrive(y, 3)
+    pred[1] = product(y, 2)
+    turn(y, 2)
+    turn(y, 3)
+    x_arrive(yo, 3)
+    for r in range(4):
+        for part in range(2):
+            w_arrive((yo, part, zs[r]))
+    p_out[...] = (pred[1] + product(yo, 2)).astype(BF16).reshape(2, rows, half)
+    for slot in range(2):
+        push(p_out.at[slot], p_in.at[slot], sem_p.at[slot], xn_dev)
+    pred[0] += product(yo, 0)
 
     for r in range(1, 4):
         for part in range(2):
@@ -285,84 +308,56 @@
         place = (h % 2) * HD
         att_half[h // 2, :, place : place + HD] = done
     push(att_half.at[pc], att_peer, sem_att.at[0], mate)
-    relay(3)
-
-    for r in range(4):
-        w_arrive((qx, 1, zs[r]))
-    pred[...] += jnp.dot(xn[qx], w_block(qx), preferred_element_type=F32)
-    for r in range(4):
-        w_arrive((qy, 0, zs[r]))
-    pred[...] += jnp.dot(xn[qy], w_block(qy), preferred_element_type=F32)
+
+    def scale_rows(slot, attended):
+        arrive(p_in.at[slot], sem_p.at[slot])
+        factor = jnp.concatenate([inv[slot]] * (half // 128), axis=1)
+        raw = pred[0, slot * rows : (slot + 1) * rows, :] + p_in[slot].astype(F32)
+        gap = raw * factor - attended.astype(F32)
+        s_all[slot] = (gap * token_total ** (-0.5) * factor).astype(BF16)
+        push(s_all.at[slot], s_all.at[slot + 2], sem_s.at[slot], xn_dev)
+
+    scale_rows(0, att_half[c])
     arrive(att_peer, sem_att.at[0])
-    for r in range(4):
+    arrive(inv.at[1], sem_inv.at[0])
+    scale_rows(1, att_peer[...])
+    turn(yo, 2)
+    turn(yo, 3)
+
+    def grad(at_y, first):
+        return jnp.dot(
+            xt[at_y, :, first * rows : (first + 2) * rows],
+            s_all[first : first + 2].reshape(2 * rows, half),
+            preferred_element_type=F32,
+        ).reshape(2, 4, piece, half)
+
+    grad_f[yo] = grad(yo, 0)
+    grad_f[y] = grad(y, 0)
+    for slot in range(2):
+        arrive(s_all.at[slot + 2], sem_s.at[slot])
+    s_y[...] = (grad_f[yo] + grad(yo, 2)).astype(BF16)
+    order = (3, 2, 1, 0)
+    for r in order:
         for part in range(2):
-            w_arrive((qd, part, zs[r]))
-    predicted = pred[...] + jnp.dot(xn[qd], w_block(qd), preferred_element_type=F32)
-    attended = jnp.concatenate([att_half[c], att_peer[...]], axis=0).astype(F32)
-    scaled = ((predicted - attended) * token_total ** (-0.5)).astype(BF16)
-
-    def grad(at):
-        return jnp.dot(xt[at], scaled, preferred_element_type=F32).reshape(2, 4, piece, half)
-
-    def send_diagonal(g):
-        push(s_d.at[0, g], r_dy.at[g], sem_dy.at[g], yn_dev)
-        push(s_d.at[1, g], r_dx.at[g], sem_dx.at[g], xn_dev)
-
-    def send_direct(g):
-        push(s_x.at[1, g], r_x.at[1, g], sem_rx.at[1, g], xn_dev)
-        push(s_y.at[0, g], r_y.at[0, g], sem_ry.at[0, g], yn_dev)
-
-    def send_joined(g):
-        arrive(r_dy.at[g], sem_dy.at[g])
-        s_x[0, g] = (gx_f[g] + r_dy[g].astype(F32)).astype(BF16)
-        push(s_x.at[0, g], r_x.at[0, g], sem_rx.at[0, g], xn_dev)
-        arrive(r_dx.at[g], sem_dx.at[g])
-        s_y[1, g] = (gy_f[g] + r_dx[g].astype(F32)).astype(BF16)
-        push(s_y.at[1, g], r_y.at[1, g], sem_ry.at[1, g], yn_dev)
+            at = (part, zs[r])
+            push(s_y.at[at], r_y.at[at], sem_ry.at[at], yn_dev)
+    grad_f[y] += grad(y, 2)
 
     def column_sum(part, g):
-        arrive(r_x.at[part, g], sem_rx.at[part, g])
         arrive(r_y.at[part, g], sem_ry.at[part, g])
-        return own_f[part, g] + r_x[part, g].astype(F32) + r_y[part, g].astype(F32)
-
-    def send_column(r):
+        return grad_f[y, part, g] + r_y[part, g].astype(F32)
+
+    for r in order[:3]:
         g = zs[r]
         for part in range(2):
             s_z[part, g] = column_sum(part, g).astype(BF16)
         push(s_z.at[c, g], r_z.at[z, c], sem_rz.at[z, c], z_dev[r])
         push(s_z.at[pc, g], r_z.at[z, c], sem_rz.at[z, c], z_mate[r])
-
-    order = (3, 2, 1, 0)
-    g = [zs[r] for r in order]
-    s_d[...] = grad(qd).astype(BF16)
-    send_diagonal(g[0])
-    send_diagonal(g[1])
-    block = grad(qx)
-    gx_f[...] = block[0]
-    s_x[1] = block[1].astype(BF16)
-    block = grad(qy)
-    gy_f[...] = block[1]
-    s_y[0] = block[0].astype(BF16)
-    send_direct(g[0])
-    own_f[...] = grad(q)
-    send_joined(g[0])
-    send_diagonal(g[2])
-    send_direct(g[1])
-    send_joined(g[1])
-    send_diagonal(g[3])
-    send_direct(g[2])
-    send_column(order[0])
-    send_joined(g[2])
-    send_direct(g[3])
-    send_column(order[1])
-    send_joined(g[3])
-    send_column(order[2])
-
     for part in range(2):
-        own_f[part, z] = column_sum(part, z)
-    s_z[pc, z] = own_f[pc, z].astype(BF16)
+        grad_f[y, part, z] = column_sum(part, z)
+    s_z[pc, z] = grad_f[y, pc, z].astype(BF16)
     push(s_z.at[pc, z], r_z.at[z, c], sem_rz.at[z, c], mate)
-    total = own_f[c, z]
+    total = grad_f[y, c, z]
     for r in range(1, 4):
         arrive(r_z.at[zs[r], c], sem_rz.at[zs[r], c])
         total = total + r_z[zs[r], c].astype(F32)
@@ -395,34 +390,30 @@
         in_specs=[vmem] * 5 + [smem] * 2,
         out_specs=(vmem, vmem),
         scratch_shapes=[
-            pltpu.VMEM((rows, width), BF16),
-            pltpu.VMEM((4,) + quarter, BF16),
+            pltpu.VMEM((2, 4, rows, depth), BF16),
+            pltpu.VMEM((2, depth, 4 * rows), BF16),
+            pltpu.VMEM((2,) + quarter, BF16),
             pltpu.VMEM((2, 4, rows, HD), BF16),
-            pltpu.VMEM((4, 2 * rows, depth), BF16),
-            pltpu.VMEM((4, depth, 2 * rows), BF16),
-            pltpu.VMEM((2 * rows, half), F32),
+            pltpu.VMEM((2, rows, 128), F32),
+            pltpu.VMEM((2, 2 * rows, half), F32),
+            pltpu.VMEM((2, rows, half), BF16),
+            pltpu.VMEM((2, rows, half), BF16),
+            pltpu.VMEM((4, rows, half), BF16),
             pltpu.VMEM((2, rows, half), BF16),
             pltpu.VMEM((rows, half), BF16),
-            pltpu.VMEM(quarter, F32),
-            pltpu.VMEM(quarter[1:], F32),
-            pltpu.VMEM(quarter[1:], F32),
+            pltpu.VMEM((2,) + quarter, F32),
             pltpu.VMEM(quarter, BF16),
             pltpu.VMEM(quarter, BF16),
             pltpu.VMEM(quarter, BF16),
-            pltpu.VMEM(quarter, BF16),
-            pltpu.VMEM(quarter[1:], BF16),
-            pltpu.VMEM(quarter[1:], BF16),
-            pltpu.VMEM(quarter, BF16),
-            pltpu.VMEM(quarter, BF16),
             pltpu.VMEM((4, 2, piece, half), BF16),
-            dma((80,)),
-            dma((4, 2, 4)),
+            dma((64,)),
+            dma((2, 2, 4)),
+            dma((2, 4)),
             dma((2, 4)),
             dma((1,)),
             dma((1,)),
-            dma((4,)),
-            dma((4,)),
-            dma((2, 4)),
+            dma((2,)),
+            dma((2,)),
             dma((2, 4)),
             dma((4, 2)),
         ],

time: 54.1 us -> 53.6 us (level)
  no operation moved by 1% of the time
where the time goes in v2:
time: 53.6 us; the launch traced here: 53.4 us
  Pallas kernels  50.5 us (94%)
  local copies, waits for them, and re-layouts  2.3 us (4%)
  between operations  0.65 us (1%)
    pallas_call x1, Pallas kernels, local_fused(): pl.pallas_call(functools.partial(fused_kernel, token_total), out_shape=(j...  50.5 us
    unnamed x4, local copies, waits for them, and re-layouts  2.3 us

profile of v2, /device:TPU:0, one launch (start us, length us, event | category | flops | bytes accessed | tf_op | source)
XLA Modules:
  0.0 53.4 jit_solution(2979592065243584366)
XLA Ops:
  0.6 50.5 %distill.1 = (bf16[128,512]{1,0:T(8,128)(2,1)}, f32[112,512]{1,0:T(8,128)}) custom-call(bf16[128,3584]{1,0:T(8,128)(2,1)} %x_ref.1, bf16[112,512]{1,0:T(8,128)(2,1)} %w_ref.1, bf16[128,512]{1,0:T(8,128)(2,1)} %q_ref.1, bf16[128,128]{1,0:T(8,128)(2,1)} %k_ref.1, bf16[128,128]{1,0:T(8,128)(2,1)} %v_ref.1, s32[1,4]{1,0:T(1,128)} %len_ref.1, s32[1,4]{1,0:T(1,128)} %asg_ref.1), custom_call_target="tpu_custom_call" | custom-call | tf_op jit(solution)/shard_map/distill/pallas_call | solution.py:384
  51.1 0.0 copy-start
  51.1 1.6 %copy.11 = bf16[128,512]{1,0:T(8,128)(2,1)} copy(bf16[128,512]{1,0:T(8,128)(2,1)} %get-tuple-element.4) | data formatting | bytes 262144
  52.7 0.0 copy-done
  52.7 0.7 %copy.12 = f32[112,512]{1,0:T(8,128)} copy(f32[112,512]{1,0:T(8,128)S(1)} %copy-done) | data formatting | bytes 458752
Async XLA Ops:
  51.1 1.6 %copy-start = (f32[112,512]{1,0:T(8,128)S(1)}, f32[112,512]{1,0:T(8,128)}, u32[]{:S(2)}) copy-start(f32[112,512]{1,0:T(8,128)} %get-tuple-element.5) | copy-start | bytes 688132

commit v3 on v2

--- a/solution.py
+++ b/solution.py
@@ -127,7 +127,7 @@
     att_ref, out_ref,
     xs, xt, w_all, kv_all, inv, pred, p_out, p_in, s_all, att_half, att_peer,
     grad_f, s_y, r_y, s_z, r_z,
-    send, sem_w, sem_kv, sem_x, sem_inv, sem_att, sem_p, sem_s, sem_ry, sem_rz,
+    send, send_z, sem_w, sem_kv, sem_x, sem_inv, sem_att, sem_p, sem_s, sem_ry, sem_rz,
 ):
     rows = q_ref.shape[0]
     piece = w_ref.shape[0]
@@ -146,13 +146,32 @@
     z_dev = [(dp, zs[r]) for r in range(4)]
     z_mate = [(dp + 1 - 2 * c, zs[r]) for r in range(4)]
 
-    peers = [mate, xn_dev, yn_dev] + z_dev[1:] + z_mate[1:]
+    below, above = (dp, (z + 3) % 4), (dp, (z + 1) % 4)
     barrier = pltpu.get_barrier_semaphore()
-    for dev in peers:
+    for dev in (mate, xn_dev, yn_dev):
         pl.semaphore_signal(barrier, inc=1, device_id=dev, device_id_type=MESH)
-    pl.semaphore_wait(barrier, len(peers))
+    for present, dev in ((z > 0, below), (z < 3, above)):
+
+        @pl.when(present)
+        def _():
+            pl.semaphore_signal(barrier, inc=1, device_id=dev, device_id_type=MESH)
+
+    pl.semaphore_wait(barrier, 3 + jnp.minimum(z, 1) + jnp.minimum(3 - z, 1))
 
     sent = []
+    sent_when = []
+
+    def push_when(present, src, dst, rsem, dev):
+        copy = pltpu.make_async_remote_copy(
+            src_ref=src, dst_ref=dst, send_sem=send_z.at[len(sent_when)], recv_sem=rsem,
+            device_id=dev, device_id_type=MESH,
+        )
+        pl.when(present)(copy.start)
+        sent_when.append((present, copy))
+
+    def both_ways(src, dst, rsem):
+        push_when(z > 0, src, dst, rsem, below)
+        push_when(z < 3, src, dst, rsem, above)
 
     def push(src, dst, rsem, dev):
         copy = pltpu.make_async_remote_copy(
@@ -186,7 +205,7 @@
     mine, other = (y, c, z), (y, pc, z)
     own_half = w_ref.at[:, cols(c)]
     push(w_ref.at[:, cols(pc)], w_all.at[mine], sem_w.at[mine], mate)
-    push(own_half, w_all.at[mine], sem_w.at[mine], z_dev[1])
+    both_ways(own_half, w_all.at[mine], sem_w.at[mine])
     push(own_half, w_all.at[mine], sem_w.at[mine], yn_dev)
     x_push(y, 1 - x, 2, xn_dev)
     x_push(yo, 1 - x, 2, xn_dev)
@@ -194,14 +213,8 @@
     x_push(yo, x, 1, mate)
     w_all[mine] = w_ref[:, cols(c)]
     w_arrive(other)
-    w_push(other, z_dev[1])
+    both_ways(w_all.at[other], w_all.at[other], sem_w.at[other])
     w_push(other, yn_dev)
-    for r in (2, 3):
-        push(own_half, w_all.at[mine], sem_w.at[mine], z_dev[r])
-        w_push(other, z_dev[r])
-    for r in (1, 2, 3):
-        push(k_ref, kv_all.at[0, z], sem_kv.at[0, z], z_dev[r])
-        push(v_ref, kv_all.at[1, z], sem_kv.at[1, z], z_dev[r])
     kv_all[0, z] = k_ref[...]
     kv_all[1, z] = v_ref[...]
     xs[y, 0] = x_ref[:, width(y, x)]
@@ -218,11 +231,36 @@
 
     push(inv.at[0], inv.at[1], sem_inv.at[0], mate)
 
-    def forward(r):
+    def sources(k):
+        return (
+            (z >= k, (z >= k) & (z < 3), (z + 4 - k) % 4, above),
+            (z + k <= 3, (z + k <= 3) & (z > 0), (z + k) % 4, below),
+        )
+
+    def forward(k):
         for part in range(2):
-            at = (y, part, zs[r])
-            w_arrive(at)
-            w_push(at, yn_dev)
+            for present, onward, chunk, dev in sources(k):
+                at = (y, part, chunk)
+
+                @pl.when(present)
+                def _():
+                    w_arrive(at)
+
+                if k < 3:
+                    push_when(onward, w_all.at[at], w_all.at[at], sem_w.at[at], dev)
+                push_when(present, w_all.at[at], w_all.at[at], sem_w.at[at], yn_dev)
+
+    def kv_forward(k):
+        for part in range(2):
+            for present, onward, chunk, dev in sources(k):
+                at = (part, chunk)
+
+                @pl.when(present)
+                def _():
+                    arrive(kv_all.at[at], sem_kv.at[at])
+
+                if k < 3:
+                    push_when(onward, kv_all.at[at], kv_all.at[at], sem_kv.at[at], dev)
 
     def x_arrive(at_y, slot):
         arrive(xs.at[at_y, slot], sem_x.at[at_y, slot])
@@ -246,6 +284,8 @@
         )
 
     forward(1)
+    both_ways(k_ref, kv_all.at[0, z], sem_kv.at[0, z])
+    both_ways(v_ref, kv_all.at[1, z], sem_kv.at[1, z])
     x_arrive(y, 1)
     x_arrive(yo, 1)
     for slot in range(2):
@@ -256,7 +296,9 @@
 
     forward(2)
     x_relay(y)
+    kv_forward(1)
     forward(3)
+    kv_forward(2)
     pred[0] = product(y, 0)
     x_relay(yo)
     x_arrive(y, 3)
@@ -272,9 +314,7 @@
         push(p_out.at[slot], p_in.at[slot], sem_p.at[slot], xn_dev)
     pred[0] += product(yo, 0)
 
-    for r in range(1, 4):
-        for part in range(2):
-            arrive(kv_all.at[part, zs[r]], sem_kv.at[part, zs[r]])
+    kv_forward(3)
     ends = []
     total = 0
     for i in range(len_ref.shape[1]):
@@ -369,6 +409,8 @@
     out_ref[:, cols(pc)] = total
     for copy in sent:
         copy.wait_send()
+    for present, copy in sent_when:
+        pl.when(present)(copy.wait_send)
 
 
 def local_fused(student_in, weight, queries, keys, values, lengths, assignment):
@@ -407,6 +449,7 @@
             pltpu.VMEM(quarter, BF16),
             pltpu.VMEM((4, 2, piece, half), BF16),
             dma((64,)),
+            dma((64,)),
             dma((2, 2, 4)),
             dma((2, 4)),
             dma((2, 4)),

time: 53.6 us -> 49 us (0.914)
  Pallas kernels: 50.5 us -> 45.9 us
    pallas_call x1, Pallas kernels: 50.5 us -> 45.9 us  [local_fused(): pl.pallas_call(functools.partial(fused_kernel, token_total), out_shape=(j...]
where the time goes in v3:
time: 49 us; the launch traced here: 48.9 us
  Pallas kernels  45.9 us (94%)
  local copies, waits for them, and re-layouts  2.3 us (5%)
  between operations  0.65 us (1%)
    pallas_call x1, Pallas kernels, local_fused(): pl.pallas_call(functools.partial(fused_kernel, token_total), out_shape=(j...  45.9 us
    unnamed x4, local copies, waits for them, and re-layouts  2.3 us

profile of v3, /device:TPU:0, one launch (start us, length us, event | category | flops | bytes accessed | tf_op | source)
XLA Modules:
  0.0 48.9 jit_solution(2984593888762066464)
XLA Ops:
  0.6 45.9 %distill.1 = (bf16[128,512]{1,0:T(8,128)(2,1)}, f32[112,512]{1,0:T(8,128)}) custom-call(bf16[128,3584]{1,0:T(8,128)(2,1)} %x_ref.1, bf16[112,512]{1,0:T(8,128)(2,1)} %w_ref.1, bf16[128,512]{1,0:T(8,128)(2,1)} %q_ref.1, bf16[128,128]{1,0:T(8,128)(2,1)} %k_ref.1, bf16[128,128]{1,0:T(8,128)(2,1)} %v_ref.1, s32[1,4]{1,0:T(1,128)} %len_ref.1, s32[1,4]{1,0:T(1,128)} %asg_ref.1), custom_call_target="tpu_custom_call" | custom-call | tf_op jit(solution)/shard_map/distill/pallas_call | solution.py:426
  46.6 0.0 copy-start
  46.6 1.6 %copy.11 = bf16[128,512]{1,0:T(8,128)(2,1)} copy(bf16[128,512]{1,0:T(8,128)(2,1)} %get-tuple-element.4) | data formatting | bytes 262144
  48.2 0.0 copy-done
  48.2 0.7 %copy.12 = f32[112,512]{1,0:T(8,128)} copy(f32[112,512]{1,0:T(8,128)S(1)} %copy-done) | data formatting | bytes 458752
Async XLA Ops:
  46.6 1.6 %copy-start = (f32[112,512]{1,0:T(8,128)S(1)}, f32[112,512]{1,0:T(8,128)}, u32[]{:S(2)}) copy-start(f32[112,512]{1,0:T(8,128)} %get-tuple-element.5) | copy-start | bytes 688132
